TPU v7x, 128 devices: a whole 4x4x4 slice. The times are simulated.
128 devices in a mesh: dom: 32 (over x, y, core), grp: 4 (over z).
Axes of the slice: x: 4, y: 4, z: 4, core: 2. Of those that a mesh axis runs over, the one named last changes fastest.
Arguments:
- features: bfloat16 [262144, 256], P(('dom', 'grp')), may hold values from -6 to 6
- edge_src: int32 [2097152], P(('dom', 'grp')), may hold values from 0 to 3071, as said below
- edge_dst: int32 [2097152], P(('dom', 'grp')), may hold values from 0 to 2047, as said below
- edge_count: int32 [128], P(('dom', 'grp')), may hold values from 4096 to 16384, as said below
- halo_index: int32 [128, 128, 8], P(('dom', 'grp')), may hold values from 0 to 2047
- request_rows: int32 [128, 128, 16], P(('dom', 'grp')), may hold values from 0 to 2047, as said below
- pair_ends: int32 [262144, 2], P(('dom', 'grp')), may hold values from 0 to 2047
- labels: int32 [262144], P(('dom', 'grp')), may hold values 0 or 1
- pair_weight: float32 [262144], P(('dom', 'grp')), may hold values from 0.25 to 4
- w_self: bfloat16 [256, 256], replicated, may hold values from -0.375 to 0.375
- w_neigh: bfloat16 [256, 256], replicated, may hold values from -0.375 to 0.375
- w_hidden: bfloat16 [512, 256], replicated, may hold values from -0.25 to 0.25
- b_hidden: float32 [256], replicated, may hold values from -3 to 3
- w_out: float32 [256], replicated, may hold values from -0.375 to 0.375
Outputs:
- logits: float32 [262144], P(('dom', 'grp'))
- grad_features: float32 [262144, 256], P(('dom', 'grp'))
- grad_w_self: float32 [256, 256], replicated
- grad_w_neigh: float32 [256, 256], replicated
- grad_w_hidden: float32 [512, 256], replicated
- grad_b_hidden: float32 [256], replicated
- grad_w_out: float32 [256], replicated
Inputs may be any that keep to these rules, and one draw needn't show every extreme that they name: `edge_src`: a row of the partition's own table. `edge_dst`: a local node of the partition; slots at or past edge_count are not live and hold arbitrary values. `edge_count`: some partition has exactly 16384 live slots. `halo_index`: local rows of the sending partition; 8 to every partition, itself included. `request_rows`: local rows of the owning partition, distinct and increasing within each list of 16. `pair_ends`: rows of the shard's own received rows.
All inputs are finite; a program needn't handle non-finite values. No bound on the sum of `labels` on one device may be relied on, other than what follows from the above.
Results may differ from a plain program's by a relative error of at most 0.02.
The roundings to bfloat16 on the way count: a program that leaves them out, or rounds other values in their place, can miss the bound.
Values may be sent and summed in bfloat16 or wider, within the bound.
No kernel may reach another device: no remote copies, remote signals or barrier semaphores. Data moves between devices by JAX's collectives and lax.ppermute only.
A program may use at most 192 MiB of HBM per device.

v0:
```python
import jax
import jax.numpy as jnp
from jax import lax
from jax.sharding import PartitionSpec as P


def in_one(arrays, axis):
    vector, at, outs = (jnp.concatenate([a.reshape(-1) for a in arrays]), 0, [])
    total = lax.psum(vector, axis)
    for a in arrays:
        outs.append(total[at : at + a.size].reshape(a.shape))
        at += a.size
    return tuple(outs)


def contract_rows(left, right):
    return lax.dot_general(
        left, right, (((0,), (0,)), ((), ())), preferred_element_type=jnp.float32
    )


def per_device(
    features,
    edge_src,
    edge_dst,
    edge_count,
    halo_index,
    request_rows,
    pair_ends,
    labels,
    pair_weight,
    w_self,
    w_neigh,
    w_hidden,
    b_hidden,
    w_out,
):
    node_rows, feat_width = features.shape
    dom_count = lax.axis_size("dom")
    grp_count = lax.axis_size("grp")
    peer_count = dom_count * grp_count
    halo_len = halo_index.shape[2]
    outgoing = features[halo_index[0]]
    arrived = lax.all_to_all(outgoing, ("dom", "grp"), split_axis=0, concat_axis=0, tiled=True)
    row_table = jnp.concatenate(
        [features, arrived.reshape(peer_count * halo_len, feat_width)], axis=0
    )
    table_rows = row_table.shape[0]
    slot_total = edge_src.shape[0]
    alive_slot = jnp.arange(slot_total, dtype=jnp.int32) < edge_count[0]
    dst_index = jnp.where(alive_slot, edge_dst, node_rows)
    adjacency = (
        jnp.zeros((node_rows + 1, table_rows), jnp.float32)
        .at[dst_index, edge_src]
        .add(1.0)[:node_rows]
    )
    degree = jnp.sum(adjacency, axis=1)
    floor_deg = jnp.maximum(degree, 1.0)[:, None]
    agg_sums = jnp.dot(adjacency, row_table.astype(jnp.float32))
    aggregate = (agg_sums / floor_deg).astype(jnp.bfloat16)
    embedding = (
        jnp.dot(features, w_self, preferred_element_type=jnp.float32)
        + jnp.dot(aggregate, w_neigh, preferred_element_type=jnp.float32)
    ).astype(jnp.bfloat16)
    wanted = lax.all_to_all(
        request_rows[0], ("dom", "grp"), split_axis=0, concat_axis=0, tiled=True
    )
    req_len = wanted.shape[1]
    served = embedding[wanted]
    received = lax.all_to_all(served, ("dom", "grp"), split_axis=0, concat_axis=0, tiled=True)
    recv_rows = peer_count * req_len
    received = received.reshape(recv_rows, feat_width)
    slot_ids = jnp.arange(recv_rows, dtype=jnp.int32)[None, :]
    select_left = (pair_ends[:, 0][:, None] == slot_ids).astype(jnp.float32)
    select_right = (pair_ends[:, 1][:, None] == slot_ids).astype(jnp.float32)
    left_rows = jnp.dot(
        select_left.astype(jnp.bfloat16), received, preferred_element_type=jnp.float32
    ).astype(jnp.bfloat16)
    right_rows = jnp.dot(
        select_right.astype(jnp.bfloat16), received, preferred_element_type=jnp.float32
    ).astype(jnp.bfloat16)
    pair_input = jnp.concatenate([left_rows, right_rows], axis=1)
    pre_act = jnp.dot(pair_input, w_hidden, preferred_element_type=jnp.float32) + b_hidden
    hidden = jnp.maximum(pre_act, 0.0)
    logits = jnp.dot(hidden, w_out)
    slope_term = pair_weight * (jax.nn.sigmoid(logits) - labels.astype(jnp.float32))
    grad_out = jnp.dot(slope_term, hidden)
    delta_act = jnp.where(pre_act > 0, slope_term[:, None] * w_out[None, :], 0.0)
    grad_bias = jnp.sum(delta_act, axis=0)
    delta_b = delta_act.astype(jnp.bfloat16)
    grad_hidden = jnp.dot(pair_input.T, delta_b, preferred_element_type=jnp.float32)
    pair_grad = jnp.dot(delta_b, w_hidden.T, preferred_element_type=jnp.float32)
    received_grad = contract_rows(select_left, pair_grad[:, :feat_width]) + contract_rows(
        select_right, pair_grad[:, feat_width:]
    )
    received_grad_b = received_grad.astype(jnp.bfloat16)
    back_rows = lax.all_to_all(
        received_grad_b.reshape(peer_count, req_len, feat_width),
        ("dom", "grp"),
        split_axis=0,
        concat_axis=0,
        tiled=True,
    )
    embedding_grad = (
        jnp.zeros((node_rows, feat_width), jnp.float32)
        .at[wanted.reshape(recv_rows)]
        .add(back_rows.reshape(recv_rows, feat_width).astype(jnp.float32))
    )
    grad_b = embedding_grad.astype(jnp.bfloat16)
    grad_self = jnp.dot(features.T, grad_b, preferred_element_type=jnp.float32)
    grad_neigh = jnp.dot(aggregate.T, grad_b, preferred_element_type=jnp.float32)
    direct = jnp.dot(grad_b, w_self.T, preferred_element_type=jnp.float32)
    agg_grad = jnp.dot(grad_b, w_neigh.T, preferred_element_type=jnp.float32) / floor_deg
    table_grad = contract_rows(adjacency, agg_grad)
    returned = table_grad[node_rows:].reshape(peer_count, halo_len, feat_width)
    halo_back = lax.all_to_all(
        returned.astype(jnp.bfloat16), ("dom", "grp"), split_axis=0, concat_axis=0, tiled=True
    ).astype(returned.dtype)
    grad_features = (
        (direct + table_grad[:node_rows])
        .at[halo_index[0].reshape(peer_count * halo_len)]
        .add(halo_back.reshape(peer_count * halo_len, feat_width))
    )
    summed = in_one((grad_self, grad_neigh, grad_hidden, grad_bias, grad_out), ("dom", "grp"))
    return (logits, grad_features, summed[0], summed[1], summed[2], summed[3], summed[4])


def solution(mesh):
    in_specs = (
        P(("dom", "grp"), None),
        P(("dom", "grp")),
        P(("dom", "grp")),
        P(("dom", "grp")),
        P(("dom", "grp"), None, None),
        P(("dom", "grp"), None, None),
        P(("dom", "grp"), None),
        P(("dom", "grp")),
        P(("dom", "grp")),
        P(),
        P(),
        P(),
        P(),
        P(),
    )
    out_specs = (P(("dom", "grp")), P(("dom", "grp"), None), P(), P(), P(), P(), P())
    return jax.shard_map(
        per_device, mesh=mesh, in_specs=in_specs, out_specs=out_specs, check_vma=False
    )
```

profile of v0, /device:TPU:1, one launch (start us, length us, event | category | flops | bytes accessed | tf_op | source)
XLA Modules:
  0.0 484.7 jit_solution(14658335759810923802)
XLA Ops:
  8.7 11.5 %all-to-all-start.1 = ((s32[128,1,16]{2,1,0:T(1,128)}), s32[128,1,16]{2,1,0:T(1,128)S(1)}, u32[]{:S(2)}, u32[]{:S(2)}) async-start(s32[128,1,16]{2,1,0:T(1,128)} %bitcast.7), calls=%async_computation.1 | async-start | bytes 131072 | tf_op jit(solution)/shard_map/all_to_all | solution.py:65
  28.3 95.7 %scatter_custom_fusion.2 = f32[6294528]{0:T(1024)} fusion(s32[16384]{0:T(1024)S(1)} %broadcast_select_fusion, f32[16384]{0:T(1024)S(1)} %broadcast.84, f32[]{:T(128)} %constant.6.clone.1), kind=kCustom, calls=%fused_computation.11 | custom fusion | flops 16384 | bytes 25178116
  124.0 16.7 %slice.87 = f32[6291456]{0:T(1024)} slice(f32[6294528]{0:T(1024)} %scatter_custom_fusion.2), slice={[0:6291456]} | slice | bytes 50331648 | tf_op jit(solution)/shard_map/slice | solution.py:53
  140.8 27.1 %reshape.208 = f32[2048,3072]{1,0:T(8,128)} reshape(f32[6291456]{0:T(1024)} %slice.87) | data formatting | bytes 50331648 | tf_op jit(solution)/shard_map/slice | solution.py:53
  167.9 9.2 %reduce_sum.18 = f32[2048]{0:T(1024)S(1)} reduce(f32[2048,3072]{1,0:T(8,128)} %reshape.208, f32[]{:T(128)} %constant.6.clone.1), dimensions={1}, to_apply=%region_1.2 | reduce | flops 6289408 | bytes 25174020 | tf_op jit(solution)/shard_map/reduce_sum | solution.py:57
  177.1 5.0 %gather_fusion = bf16[1024,256]{1,0:T(8,128)(2,1)} fusion(bf16[2048,256]{1,0:T(8,128)(2,1)S(1)} %copy-done.1, s32[1024]{0:T(1024)S(1)} %broadcast_clamp_fusion.1), kind=kCustom, calls=%fused_computation | custom fusion | bytes 1052672 | tf_op jit(solution)/shard_map/gather | solution.py:43
  182.1 10.4 %all-to-all-start = ((bf16[128,8,256]{2,1,0:T(8,128)(2,1)}), bf16[128,8,256]{2,1,0:T(8,128)(2,1)S(1)}, u32[]{:S(2)}, u32[]{:S(2)}) async-start(bf16[128,8,256]{2,1,0:T(8,128)(2,1)} %bitcast.5), calls=%async_computation | async-start | bytes 1048576 | tf_op jit(solution)/shard_map/all_to_all | solution.py:44
  192.6 13.7 %all-to-all-done = bf16[128,8,256]{2,1,0:T(8,128)(2,1)S(1)} async-done(((bf16[128,8,256]{2,1,0:T(8,128)(2,1)}), bf16[128,8,256]{2,1,0:T(8,128)(2,1)S(1)}, u32[]{:S(2)}, u32[]{:S(2)}) %all-to-all-start) | async-done | bytes 524320 | tf_op jit(solution)/shard_map/all_to_all | solution.py:44
  206.3 11.9 %fusion.15 = bf16[2048,256]{1,0:T(8,128)(2,1)S(1)} fusion(f32[2048,3072]{1,0:T(8,128)} %reshape.208, bf16[1024,256]{1,0:T(8,128)(2,1)S(1)} %bitcast.67, bf16[2048,256]{1,0:T(8,128)(2,1)S(1)} %copy-done.1, f32[2048]{0:T(1024)S(1)} %broadcast_maximum_fusion), kind=kOutput, calls=%fused_computation.29 | convolution fusion | flops 3225419776 | bytes 27795456 | tf_op jit(solution)/shard_map/dot_general | solution.py:59
  218.6 9.1 %gather_fusion.1 = bf16[2048,256]{1,0:T(8,128)(2,1)} fusion(bf16[2048,256]{1,0:T(8,128)(2,1)S(1)} %fusion.12, s32[2048]{0:T(1024)S(1)} %broadcast_clamp_fusion), kind=kCustom, calls=%fused_computation.1 | custom fusion | bytes 2105344 | tf_op jit(solution)/shard_map/gather | solution.py:69
  227.7 4.1 all-to-all-start.2
  231.8 19.5 %all-to-all-done.2 = bf16[128,16,256]{2,1,0:T(8,128)(2,1)S(1)} async-done(((bf16[128,16,256]{2,1,0:T(8,128)(2,1)}), bf16[128,16,256]{2,1,0:T(8,128)(2,1)S(1)}, u32[]{:S(2)}, u32[]{:S(2)}) %all-to-all-start.2) | async-done | bytes 1048608 | tf_op jit(solution)/shard_map/all_to_all | solution.py:70
  254.2 3.1 fusion.14
  261.0 4.9 %fusion = f32[2048,256]{1,0:T(8,128)S(1)} fusion(s32[2048]{0:T(1024)S(1)} %bitcast.87, bf16[2048,512]{1,0:T(8,128)(2,1)S(1)} %fusion.33), kind=kOutput, calls=%fused_computation.7 | convolution fusion | flops 2151677952 | bytes 3153920 | tf_op jit(solution)/shard_map/dot_general | solution.py:17
  265.9 6.2 %fusion.11 = bf16[2048,256]{1,0:T(8,128)(2,1)} fusion(f32[2048,256]{1,0:T(8,128)S(1)} %fusion, s32[2048]{0:T(1024)S(1)} %bitcast.85, bf16[2048,512]{1,0:T(8,128)(2,1)S(1)} %fusion.33), kind=kOutput, calls=%fused_computation.24 | convolution fusion | flops 2152726528 | bytes 4202496 | tf_op jit(solution)/shard_map/dot_general | solution.py:17
  272.2 3.9 all-to-all-start.3
  283.1 12.5 %all-to-all-done.3 = bf16[128,16,256]{2,1,0:T(8,128)(2,1)S(1)} async-done(((bf16[128,16,256]{2,1,0:T(8,128)(2,1)}), bf16[128,16,256]{2,1,0:T(8,128)(2,1)S(1)}, u32[]{:S(2)}, u32[]{:S(2)}) %all-to-all-start.3) | async-done | bytes 1048608 | tf_op jit(solution)/shard_map/all_to_all | solution.py:97
  295.6 13.0 %scatter_custom_fusion = f32[2048,256]{1,0:T(8,128)} fusion(s32[2048]{0:T(1024)S(1)} %bitcast.83, bf16[2048,256]{1,0:T(8,128)(2,1)S(1)} %bitcast.66, f32[]{:T(128)} %constant.6.clone.1), kind=kCustom, calls=%fused_computation.34 | custom fusion | flops 1048576 | bytes 3145732 | tf_op jit(solution)/shard_map/scatter-add | solution.py:107
  312.0 12.3 %fusion.16 = f32[3072,256]{1,0:T(8,128)} fusion(f32[2048,3072]{1,0:T(8,128)} %reshape.208, bf16[2048,256]{1,0:T(8,128)(2,1)S(1)} %convert_element_type.61, bf16[256,256]{1,0:T(8,128)(2,1)S(1)} %copy-done.10, f32[2048]{0:T(1024)S(1)} %broadcast_maximum_fusion), kind=kOutput, calls=%fused_computation.30 | convolution fusion | flops 3490185216 | bytes 29499392 | tf_op jit(solution)/shard_map/dot_general | solution.py:17
  328.6 4.3 all-to-all-start.4
  332.9 3.4 convolution_add_fusion.1
  336.3 10.8 %all-to-all-done.4 = bf16[128,8,256]{2,1,0:T(8,128)(2,1)S(1)} async-done(((bf16[128,8,256]{2,1,0:T(8,128)(2,1)}), bf16[128,8,256]{2,1,0:T(8,128)(2,1)S(1)}, u32[]{:S(2)}, u32[]{:S(2)}) %all-to-all-start.4) | async-done | bytes 524320 | tf_op jit(solution)/shard_map/all_to_all | solution.py:116
  347.1 9.0 %scatter_custom_fusion.1 = f32[2048,256]{1,0:T(8,128)} fusion(f32[2048,256]{1,0:T(8,128)} %convolution_add_fusion.1, s32[1024]{0:T(1024)S(1)} %bitcast.90, bf16[128,8,256]{2,1,0:T(8,128)(2,1)S(1)} %all-to-all-done.4), kind=kCustom, calls=%fused_computation.52 | custom fusion | flops 524288 | bytes 2621440 | tf_op jit(solution)/shard_map/scatter-add | solution.py:122
  356.1 117.2 %all-reduce.2.cloned.1.call-done = f32[262656]{0:T(1024)} async-done(((f32[262656]{0:T(1024)}), f32[262656]{0:T(1024)}) %all-reduce.2.cloned.1.call-update) | async-done | bytes 1050640 | tf_op jit(solution)/shard_map/psum | solution.py:9
  (101 shorter events, 34.7 us)
Async XLA Ops:
  7.2 250.2 %copy-start = (bf16[512,256]{1,0:T(8,128)(2,1)S(1)}, bf16[512,256]{1,0:T(8,128)(2,1)}, u32[]{:S(2)}) copy-start(bf16[512,256]{1,0:T(8,128)(2,1)} %param.25) | copy-start | bytes 786436
  8.7 173.4 %all-to-all-start.1 = ((s32[128,1,16]{2,1,0:T(1,128)}), s32[128,1,16]{2,1,0:T(1,128)S(1)}, u32[]{:S(2)}, u32[]{:S(2)}) async-start(s32[128,1,16]{2,1,0:T(1,128)} %bitcast.7), calls=%async_computation.1 | async-start | bytes 131072 | tf_op jit(solution)/shard_map/all_to_all | solution.py:65
  167.9 9.2 %copy-start.1 = (bf16[2048,256]{1,0:T(8,128)(2,1)S(1)}, bf16[2048,256]{1,0:T(8,128)(2,1)}, u32[]{:S(2)}) copy-start(bf16[2048,256]{1,0:T(8,128)(2,1)} %param.14) | copy-start | bytes 3145732
  182.1 24.2 %all-to-all-start = ((bf16[128,8,256]{2,1,0:T(8,128)(2,1)}), bf16[128,8,256]{2,1,0:T(8,128)(2,1)S(1)}, u32[]{:S(2)}, u32[]{:S(2)}) async-start(bf16[128,8,256]{2,1,0:T(8,128)(2,1)} %bitcast.5), calls=%async_computation | async-start | bytes 1048576 | tf_op jit(solution)/shard_map/all_to_all | solution.py:44
  206.3 11.9 %copy-start.4 = (f32[2048,256]{1,0:T(8,128)S(1)}, f32[2048,256]{1,0:T(8,128)}, u32[]{:S(2)}) copy-start(f32[2048,256]{1,0:T(8,128)} %fusion.59) | copy-start | bytes 6291460
  206.3 11.9 %copy-start.9 = (bf16[256,256]{1,0:T(8,128)(2,1)S(1)}, bf16[256,256]{1,0:T(8,128)(2,1)}, u32[]{:S(2)}) copy-start(bf16[256,256]{1,0:T(8,128)(2,1)} %param.24) | copy-start | bytes 393220
  227.7 4.1 copy-start.15
  227.7 23.7 %all-to-all-start.2 = ((bf16[128,16,256]{2,1,0:T(8,128)(2,1)}), bf16[128,16,256]{2,1,0:T(8,128)(2,1)S(1)}, u32[]{:S(2)}, u32[]{:S(2)}) async-start(bf16[128,16,256]{2,1,0:T(8,128)(2,1)} %bitcast.65), calls=%async_computation.2 | async-start | bytes 2097152 | tf_op jit(solution)/shard_map/all_to_all | solution.py:70
  254.2 3.1 copy-start.21
  254.2 3.1 copy-start.20
  258.4 1.9 copy-start.2
  258.7 2.2 copy-start.13
  260.2 5.7 %copy-start.11 = (pred[2048,256]{1,0:T(32,128)(4,1)}, pred[2048,256]{1,0:T(32,128)(4,1)S(1)}, u32[]{:S(2)}) copy-start(pred[2048,256]{1,0:T(32,128)(4,1)S(1)} %get-tuple-element.8) | copy-start | bytes 1572868
  272.2 23.4 %all-to-all-start.3 = ((bf16[128,16,256]{2,1,0:T(8,128)(2,1)}), bf16[128,16,256]{2,1,0:T(8,128)(2,1)S(1)}, u32[]{:S(2)}, u32[]{:S(2)}) async-start(bf16[128,16,256]{2,1,0:T(8,128)(2,1)} %bitcast.69), calls=%async_computation.3 | async-start | bytes 2097152 | tf_op jit(solution)/shard_map/all_to_all | solution.py:97
  276.1 197.2 %all-reduce.2.cloned.1.call-start = ((), (), s32[]{:S(2)}) async-start(), calls=%async_computation.5 | async-start | bytes 2105344 | tf_op jit(solution)/shard_map/psum | solution.py:9
  279.1 3.8 copy-start.3
  310.3 1.7 copy-start.10
  312.0 12.3 %copy-start.8 = (f32[32,2,8,128]{3,2,1,0:T(8,128)S(1)}, f32[32,2,8,128]{3,2,1,0:T(8,128)}, u32[]{:S(2)}) copy-start(f32[32,2,8,128]{3,2,1,0:T(8,128)} %convolution_bitcast_fusion) | copy-start | bytes 786436
  324.3 1.0 copy-start.5
  324.3 1.1 copy-start.19
  325.4 7.5 %copy-start.14 = (s32[1024,1]{0,1:T(1,128)S(1)}, s32[1024,1]{0,1:T(1,128)}, u32[]{:S(2)}) copy-start(s32[1024,1]{0,1:T(1,128)} %reshape_squeeze.3) | copy-start | bytes 12292
  325.4 7.5 %copy-start.12 = (bf16[256,256]{1,0:T(8,128)(2,1)S(1)}, bf16[256,256]{1,0:T(8,128)(2,1)}, u32[]{:S(2)}) copy-start(bf16[256,256]{1,0:T(8,128)(2,1)} %param.23) | copy-start | bytes 393220
  328.6 18.5 %all-to-all-start.4 = ((bf16[128,8,256]{2,1,0:T(8,128)(2,1)}), bf16[128,8,256]{2,1,0:T(8,128)(2,1)S(1)}, u32[]{:S(2)}, u32[]{:S(2)}) async-start(bf16[128,8,256]{2,1,0:T(8,128)(2,1)} %fusion.47), calls=%async_computation.4 | async-start | bytes 1048576 | tf_op jit(solution)/shard_map/all_to_all | solution.py:116
  473.3 2.1 copy-start.7
  (5 other events, 4.4 us)
Sparse Core Ops, SparseCore 0:
  326.6 146.6 all-reduce.1
where the time goes:
time: 492 us; the launch traced here: 485 us
  waiting for transfers between devices  174 us (35%)
  other arithmetic  135 us (27%)
  local copies, waits for them, and re-layouts  71.9 us (15%)
  matrix products  54.6 us (11%)
  starting transfers between devices  34.2 us (7%)
  between operations  15.4 us (3%)
    psum x1, waiting for transfers between devices, in_one(): total = lax.psum(vector, axis)  117 us
    unnamed x4, other arithmetic  97.6 us
    slice x2, local copies, waits for them, and re-layouts, per_device(): jnp.zeros((node_rows + 1, table_rows), jnp.float32).at[dst_index, edge_src]  43.9 us
    dot_general x3, matrix products, contract_rows(): lax.dot_general(left, right, (((0,), (0,)), ((), ())), preferred_element_...  23.5 us
    all_to_all x1, waiting for transfers between devices, per_device(): lax.all_to_all(served, ('dom', 'grp'), split_axis=0, concat_axis=0, tiled...  19.5 us
    all_to_all x1, waiting for transfers between devices, per_device(): lax.all_to_all(outgoing, ('dom', 'grp'), split_axis=0, concat_axis=0, til...  13.7 us
    scatter-add x1, other arithmetic, per_device(): embedding_grad = jnp.zeros((node_rows, feat_width), jnp.float32).at[wante...  13 us
    all_to_all x1, waiting for transfers between devices, per_device(): lax.all_to_all(received_grad_b.reshape(peer_count, req_len, feat_width),...  12.5 us
  transfers between devices with their start and end apart: 6, of which 5 were waited for; matrix products, arithmetic and copies ran while one was open for 38% of the time, Pallas kernels for 0%

commit v1 on v0

--- a/solution.py
+++ b/solution.py
@@ -6,7 +6,8 @@
 
 def in_one(arrays, axis):
     vector, at, outs = (jnp.concatenate([a.reshape(-1) for a in arrays]), 0, [])
-    total = lax.psum(vector, axis)
+    terms = lax.all_gather(vector, axis, axis=0, tiled=False)
+    total = terms.sum(axis=0)
     for a in arrays:
         outs.append(total[at : at + a.size].reshape(a.shape))
         at += a.size

time: 492 us -> 1240 us (2.52)
  other arithmetic: 135 us -> 759 us
  waiting for transfers between devices: 174 us -> 298 us
    reduce_sum x0 -> x1, other arithmetic: none -> 625 us  [in_one(): total = terms.sum(axis=0)]
    all_gather x0 -> x1, waiting for transfers between devices: none -> 241 us  [in_one(): terms = lax.all_gather(vector, axis, axis=0, tiled=False)]
    psum x1 -> x0, waiting for transfers between devices: 117 us -> none  [in_one(): total = lax.psum(vector, axis)]
  transfers between devices with their start and end apart: 6 -> 6, of which waited for: 5 -> 5; matrix products, arithmetic and copies ran while one was open for 38% -> 16% of each run, Pallas kernels for 0% -> 0%
where the time goes in v1:
time: 1240 us
  other arithmetic  759 us (61%)
  waiting for transfers between devices  298 us (24%)
  local copies, waits for them, and re-layouts  73.8 us (6%)
  matrix products  54.8 us (4%)
  starting transfers between devices  34 us (3%)
  between operations  15.6 us (1%)
    reduce_sum x1, other arithmetic, in_one(): total = terms.sum(axis=0)  625 us
    all_gather x1, waiting for transfers between devices, in_one(): terms = lax.all_gather(vector, axis, axis=0, tiled=False)  241 us
    unnamed x4, other arithmetic  97.6 us
    slice x2, local copies, waits for them, and re-layouts, per_device(): jnp.zeros((node_rows + 1, table_rows), jnp.float32).at[dst_index, edge_src]  43.9 us
  transfers between devices with their start and end apart: 6, of which 5 were waited for; matrix products, arithmetic and copies ran while one was open for 16% of the time, Pallas kernels for 0%

profile of v1, /device:TPU:1, one launch (start us, length us, event | category | flops | bytes accessed | tf_op | source)
XLA Modules:
  0.0 1235.3 jit_solution(4298188149215909328)
XLA Ops:
  8.7 11.5 all-to-all-start.1
  28.4 5.0 gather_fusion
  33.4 95.7 %scatter_custom_fusion.2 = f32[6294528]{0:T(1024)} fusion(s32[16384]{0:T(1024)S(1)} %broadcast_select_fusion, f32[16384]{0:T(1024)S(1)} %broadcast.84, f32[]{:T(128)} %constant.6.clone.1), kind=kCustom, calls=%fused_computation.11 | custom fusion | flops 16384 | bytes 25178116
  129.1 16.7 %slice.87 = f32[6291456]{0:T(1024)} slice(f32[6294528]{0:T(1024)} %scatter_custom_fusion.2), slice={[0:6291456]} | slice | bytes 50331648 | tf_op jit(solution)/shard_map/slice | solution.py:54
  145.8 27.2 %reshape.208 = f32[2048,3072]{1,0:T(8,128)} reshape(f32[6291456]{0:T(1024)} %slice.87) | data formatting | bytes 50331648 | tf_op jit(solution)/shard_map/slice | solution.py:54
  173.0 9.1 reduce_sum.27
  182.2 10.4 all-to-all-start
  192.7 13.7 %all-to-all-done = bf16[128,8,256]{2,1,0:T(8,128)(2,1)S(1)} async-done(((bf16[128,8,256]{2,1,0:T(8,128)(2,1)}), bf16[128,8,256]{2,1,0:T(8,128)(2,1)S(1)}, u32[]{:S(2)}, u32[]{:S(2)}) %all-to-all-start) | async-done | bytes 524320 | tf_op jit(solution)/shard_map/all_to_all | solution.py:45
  206.3 11.9 fusion.15
  218.7 9.1 gather_fusion.1
  227.7 4.1 all-to-all-start.2
  231.9 19.5 %all-to-all-done.2 = bf16[128,16,256]{2,1,0:T(8,128)(2,1)S(1)} async-done(((bf16[128,16,256]{2,1,0:T(8,128)(2,1)}), bf16[128,16,256]{2,1,0:T(8,128)(2,1)S(1)}, u32[]{:S(2)}, u32[]{:S(2)}) %all-to-all-start.2) | async-done | bytes 1048608 | tf_op jit(solution)/shard_map/all_to_all | solution.py:71
  260.5 4.9 fusion
  265.5 6.2 fusion.11
  271.6 3.9 all-to-all-start.3
  281.1 14.0 %all-to-all-done.3 = bf16[128,16,256]{2,1,0:T(8,128)(2,1)S(1)} async-done(((bf16[128,16,256]{2,1,0:T(8,128)(2,1)}), bf16[128,16,256]{2,1,0:T(8,128)(2,1)S(1)}, u32[]{:S(2)}, u32[]{:S(2)}) %all-to-all-start.3) | async-done | bytes 1048608 | tf_op jit(solution)/shard_map/all_to_all | solution.py:98
  295.1 13.0 %scatter_custom_fusion = f32[2048,256]{1,0:T(8,128)} fusion(s32[2048]{0:T(1024)S(1)} %bitcast.83, bf16[2048,256]{1,0:T(8,128)(2,1)S(1)} %bitcast.66, f32[]{:T(128)} %constant.6.clone.1), kind=kCustom, calls=%fused_computation.34 | custom fusion | flops 1048576 | bytes 3145732 | tf_op jit(solution)/shard_map/scatter-add | solution.py:108
  311.4 5.7 reshape.253
  317.3 13.3 %fusion.16 = f32[3072,256]{1,0:T(8,128)} fusion(f32[2048,3072]{1,0:T(8,128)} %reshape.208, bf16[2048,256]{1,0:T(8,128)(2,1)S(1)} %convert_element_type.61, bf16[256,256]{1,0:T(8,128)(2,1)S(1)} %copy-done.8, f32[2048]{0:T(1024)S(1)} %broadcast_maximum_fusion), kind=kOutput, calls=%fused_computation.30 | convolution fusion | flops 3490185216 | bytes 29499392 | tf_op jit(solution)/shard_map/dot_general | solution.py:18
  332.8 4.1 all-to-all-start.4
  340.3 10.5 all-to-all-done.4
  350.8 9.0 scatter_custom_fusion.1
  359.7 240.6 %all-gather.4.cloned.1.call-done = f32[128,1,262656]{2,1,0:T(1,128)} async-done(((f32[1,1,262656]{2,1,0:T(1,128)}), f32[128,1,262656]{2,1,0:T(1,128)}) %all-gather.4.cloned.1.call-update) | async-done | bytes 134479888 | tf_op jit(solution)/shard_map/all_gather | solution.py:9
  600.3 624.5 %reduce_sum.29 = f32[262656]{0:T(1024)S(1)} reduce(f32[128,1,262656]{2,1,0:T(1,128)} %all-gather.4.cloned.1.call-done, f32[]{:T(128)} %constant.6.clone.1), dimensions={0,1}, to_apply=%region_5.6 | reduce | flops 33357312 | bytes 135530496 | tf_op jit(solution)/shard_map/reduce_sum | solution.py:10
  (97 shorter events, 36.3 us)
Async XLA Ops:
  7.2 250.3 %copy-start = (bf16[512,256]{1,0:T(8,128)(2,1)S(1)}, bf16[512,256]{1,0:T(8,128)(2,1)}, u32[]{:S(2)}) copy-start(bf16[512,256]{1,0:T(8,128)(2,1)} %param.25) | copy-start | bytes 786436
  8.7 173.5 %all-to-all-start.1 = ((s32[128,1,16]{2,1,0:T(1,128)}), s32[128,1,16]{2,1,0:T(1,128)S(1)}, u32[]{:S(2)}, u32[]{:S(2)}) async-start(s32[128,1,16]{2,1,0:T(1,128)} %bitcast.7), calls=%async_computation.1 | async-start | bytes 131072 | tf_op jit(solution)/shard_map/all_to_all | solution.py:66
  20.8 7.6 copy-start.2
  182.2 24.2 %all-to-all-start = ((bf16[128,8,256]{2,1,0:T(8,128)(2,1)}), bf16[128,8,256]{2,1,0:T(8,128)(2,1)S(1)}, u32[]{:S(2)}, u32[]{:S(2)}) async-start(bf16[128,8,256]{2,1,0:T(8,128)(2,1)} %bitcast.5), calls=%async_computation | async-start | bytes 1048576 | tf_op jit(solution)/shard_map/all_to_all | solution.py:45
  206.3 11.9 copy-start.5
  206.3 11.9 copy-start.7
  227.7 4.1 copy-start.13
  227.7 23.7 %all-to-all-start.2 = ((bf16[128,16,256]{2,1,0:T(8,128)(2,1)}), bf16[128,16,256]{2,1,0:T(8,128)(2,1)S(1)}, u32[]{:S(2)}, u32[]{:S(2)}) async-start(bf16[128,16,256]{2,1,0:T(8,128)(2,1)} %bitcast.65), calls=%async_computation.2 | async-start | bytes 2097152 | tf_op jit(solution)/shard_map/all_to_all | solution.py:71
  254.3 3.1 copy-start.18
  254.3 3.1 copy-start.17
  257.4 1.0 copy-start.19
  257.5 1.0 copy-start.16
  258.4 1.3 copy-start.3
  258.8 1.7 copy-start.11
  259.8 5.7 copy-start.9
  271.6 23.4 %all-to-all-start.3 = ((bf16[128,16,256]{2,1,0:T(8,128)(2,1)}), bf16[128,16,256]{2,1,0:T(8,128)(2,1)S(1)}, u32[]{:S(2)}, u32[]{:S(2)}) async-start(bf16[128,16,256]{2,1,0:T(8,128)(2,1)} %bitcast.69), calls=%async_computation.3 | async-start | bytes 2097152 | tf_op jit(solution)/shard_map/all_to_all | solution.py:98
  275.5 324.8 %all-gather.4.cloned.1.call-start = ((), (), s32[]{:S(2)}) async-start(), calls=%async_computation.5 | async-start | bytes 135530496 | tf_op jit(solution)/shard_map/all_gather | solution.py:9
  277.0 3.8 copy-start.4
  310.3 1.0 copy-start.6
  311.3 5.8 copy-start.12
  311.3 6.0 copy-start.8
  330.6 6.3 copy-start.10
  332.8 18.0 %all-to-all-start.4 = ((bf16[128,8,256]{2,1,0:T(8,128)(2,1)}), bf16[128,8,256]{2,1,0:T(8,128)(2,1)S(1)}, u32[]{:S(2)}, u32[]{:S(2)}) async-start(bf16[128,8,256]{2,1,0:T(8,128)(2,1)} %fusion.47), calls=%async_computation.4 | async-start | bytes 1048576 | tf_op jit(solution)/shard_map/all_to_all | solution.py:117
  1224.9 3.2 copy-start.1
  (2 other events, 1.5 us)
Sparse Core Ops, SparseCore 0:
  317.2 283.0 all-gather.3
